TPU v7x, 32 devices: a whole 2x2x4 slice. The times are simulated.
32 devices in a mesh: grp: 8 (over y, x, core), dom: 4 (over z).
Axes of the slice: x: 2, y: 2, z: 4, core: 2. Of those that a mesh axis runs over, the one named last changes fastest.
Arguments:
- surplus: float32 [128, 512, 512], P('grp', 'dom'), may hold values from -0.4 to 0.4
- block_ids: int32 [128, 512], P('grp', 'dom'), may hold values from 0 to 4095, as said below
- coef: int32 [128], P('grp'), may hold values from -4 to 6, as said below
Outputs:
- updated: float32 [128, 512, 512], P('grp', 'dom')
Inputs may be any that keep to these rules, and one draw needn't show every extreme that they name: `block_ids`: for each grid, the slots in columns d * 128 to (d + 1) * 128 - 1 hold 128 different numbers from d * 1024 to (d + 1) * 1024 - 1. `coef`: each coefficient is one of 1, -4, 6.
All inputs are finite; a program needn't handle non-finite values.
Results may differ from a plain program's by a relative error of at most 0.000071.
Values sent between devices are 32-bit elements; how exact they have to be, the bound alone decides.
A program may use at most 64 MiB of HBM per device.

v0:
```python
import jax
import jax.numpy as jnp
from jax import lax
from jax.sharding import PartitionSpec as P

NBD = 1024


def local(surplus, block_ids, coef):
    offset = lax.axis_index("dom") * NBD
    local_ids = block_ids - offset
    columns = lax.broadcasted_iota(jnp.int32, (1, 1, NBD), 2)
    onehot = (local_ids[:, :, None] == columns).astype(jnp.float32)
    scaled = surplus * coef.astype(jnp.float32)[:, None, None]
    partial_sum = jnp.einsum("gkn,gkb->nb", onehot, scaled, precision=lax.Precision.HIGHEST)
    combined = lax.psum(partial_sum, "grp")
    return jnp.einsum("gkn,nb->gkb", onehot, combined, precision=lax.Precision.HIGHEST)


def solution(mesh):
    return jax.shard_map(
        local,
        mesh=mesh,
        in_specs=(P("grp", "dom", None), P("grp", "dom"), P("grp")),
        out_specs=P("grp", "dom", None),
        check_vma=False,
    )
```

profile of v0, /device:TPU:0, one launch (start us, length us, event | category | flops | bytes accessed | tf_op | source)
XLA Modules:
  0.0 106.6 jit_solution(6642148042508687133)
XLA Ops:
  6.5 0.0 all-reduce.2.cloned.1.call-start
  6.5 0.7 convert_element_type.4
  7.2 0.7 broadcast_subtract_fusion
  7.9 16.8 %fusion.7 = f32[1024,512]{1,0:T(8,128)} fusion(f32[16,128,512]{2,1,0:T(8,128)} %param.3, f32[16]{0:T(128)S(1)} %convert_element_type.4, s32[16,128]{1,0:T(8,128)S(1)} %broadcast_subtract_fusion), kind=kOutput, calls=%fused_computation.8 | convolution fusion | flops 12888047616 | bytes 6299712 | tf_op jit(solution)/shard_map/gkn,gkb->nb/dot_general | solution.py:15
  24.7 0.0 all-reduce.2.cloned.1.call-update
  24.7 64.6 %all-reduce.2.cloned.1.call-done = f32[1024,512]{1,0:T(8,128)} async-done(((f32[1024,512]{1,0:T(8,128)}), f32[1024,512]{1,0:T(8,128)}) %all-reduce.2.cloned.1.call-update) | async-done | bytes 2097168 | tf_op jit(solution)/shard_map/psum | solution.py:16
  89.3 10.4 %fusion = f32[16,128,512]{2,1,0:T(8,128)} fusion(s32[16,128]{1,0:T(8,128)S(1)} %broadcast_subtract_fusion, f32[1024,512]{1,0:T(8,128)} %all-reduce.2.cloned.1.call-done), kind=kOutput, calls=%fused_computation.1 | convolution fusion | flops 12886999040 | bytes 6299648 | tf_op jit(solution)/shard_map/gkn,nb->gkb/dot_general | solution.py:17
Async XLA Ops:
  6.5 82.8 %all-reduce.2.cloned.1.call-start = ((), (), s32[]{:S(2)}) async-start(), calls=%async_computation | async-start | bytes 4194304 | tf_op jit(solution)/shard_map/psum | solution.py:16
Sparse Core Ops, SparseCore 0:
  24.8 64.4 all-reduce.1
where the time goes:
time: 107 us
  waiting for transfers between devices  64.7 us (60%)
  matrix products  27.2 us (25%)
  between operations  13.4 us (13%)
  other arithmetic  1.36 us (1%)
    psum x1, waiting for transfers between devices, local(): combined = lax.psum(partial_sum, 'grp')  64.6 us
    dot_general x1, matrix products, local(): jnp.einsum('gkn,gkb->nb', onehot, scaled, precision=lax.Precision.HIGHEST)  16.8 us
    dot_general x1, matrix products, local(): jnp.einsum('gkn,nb->gkb', onehot, combined, precision=lax.Precision.HIGHEST)  10.4 us
  transfers between devices with their start and end apart: 1, of which 1 were waited for; matrix products, arithmetic and copies ran while one was open for 0% of the time, Pallas kernels for 0%

commit v1 on v0

--- a/solution.py
+++ b/solution.py
@@ -1,9 +1,253 @@
+import functools
+
 import jax
 import jax.numpy as jnp
 from jax import lax
+from jax.experimental import pallas as pl
+from jax.experimental.pallas import tpu as pltpu
 from jax.sharding import PartitionSpec as P
 
 NBD = 1024
+CORES = 2
+SIDE = 2
+STREAMS = 2
+LOADS = 4
+MESH = pl.DeviceIdType.MESH
+DIAG, XN, YN, OWN = 0, 1, 2, 3
+F32, BF16 = jnp.float32, jnp.bfloat16
+
+
+def kernel(ids_ref, coef_ref, x_ref, out_ref, xf, xhi, xlo, w, oh, p, rd, rrel,
+           rx, ry, cc, chi, clo, idst, load_sem, ss, rs):
+    grids, k, blk = x_ref.shape
+    part = rd.shape[1]
+    rows = part // STREAMS
+    h = rows // 2
+    per = grids // LOADS
+
+    me = lax.axis_index("grp")
+    core = lax.rem(me, CORES)
+    chip = me // CORES
+    x, y = lax.rem(chip, SIDE), chip // SIDE
+    ox, oy = 1 - x, 1 - y
+
+    def index_of(cy, cx):
+        return cy * SIDE + cx
+
+    chips = {DIAG: index_of(oy, ox), XN: index_of(y, ox), YN: index_of(oy, x), OWN: chip}
+    partner = chip * CORES + (1 - core)
+    xn, yn = chips[XN] * CORES + core, chips[YN] * CORES + core
+    origin = lax.axis_index("dom") * NBD
+
+    def base(q, other):
+        c = 1 - core if other else core
+        return origin + (chips[q] * CORES + c) * part
+
+    loads = []
+    for n in range(LOADS):
+        span = pl.ds(n * per, per)
+        copy = pltpu.make_async_copy(x_ref.at[span], xf.at[span], load_sem.at[n])
+        copy.start()
+        loads.append(copy)
+
+    barrier = pltpu.get_barrier_semaphore()
+    for device in (partner, xn, yn):
+        pl.semaphore_signal(barrier, inc=1, device_id={"grp": device}, device_id_type=MESH)
+
+    row = lax.broadcasted_iota(jnp.int32, (part, k), 0)
+    lane = lax.broadcasted_iota(jnp.int32, (k, part), 1)
+
+    def build_w(q):
+        for other in (0, 1):
+            shifted = row + base(q, other)
+            for g in range(grids):
+                value = coef_ref[g].astype(F32)
+                hit = ids_ref[g:g + 1, :] == shifted
+                w[other * part:(other + 1) * part, g * k:(g + 1) * k] = jnp.where(hit, value, 0.0).astype(BF16)
+
+    def build_oh(q):
+        for other in (0, 1):
+            shifted = lane + base(q, other)
+            for g in range(grids):
+                hit = idst[:, g:g + 1] == shifted
+                oh[q, g * k:(g + 1) * k, other * part:(other + 1) * part] = jnp.where(hit, 1.0, 0.0).astype(BF16)
+
+    def partial(q):
+        p[q] = jnp.dot(w[...], xhi[...], preferred_element_type=F32) + jnp.dot(
+            w[...], xlo[...], preferred_element_type=F32)
+
+    started = []
+    counter = [0]
+
+    def send(src, dst, device):
+        n = counter[0]
+        counter[0] += 1
+        copy = pltpu.make_async_remote_copy(
+            src_ref=src, dst_ref=dst, send_sem=ss.at[n], recv_sem=rs.at[n],
+            device_id={"grp": device}, device_id_type=MESH)
+        copy.start()
+        started.append(copy)
+        return copy
+
+    build_w(DIAG)
+    for n, copy in enumerate(loads):
+        copy.wait()
+        for g in range(n * per, (n + 1) * per):
+            value = xf[g]
+            high = value.astype(BF16)
+            xhi[g * k:(g + 1) * k, :] = high
+            xlo[g * k:(g + 1) * k, :] = (value - high.astype(F32)).astype(BF16)
+
+    pl.semaphore_wait(barrier, 3)
+
+    def pair(q):
+        return send(p.at[q, pl.ds(part, part)], rd.at[q], partner)
+
+    def add_pair(q, copy):
+        copy.wait_recv()
+        p[q, 0:part] = p[q, 0:part] + rd[q]
+
+    def piece(ref, q, s, half):
+        return ref.at[q, pl.ds(s * rows + half * h, h)]
+
+    partial(DIAG)
+    pair_d = pair(DIAG)
+    build_w(XN)
+    partial(XN)
+    pair_x = pair(XN)
+    add_pair(DIAG, pair_d)
+    relay_x, relay_y = [], []
+    for s in range(STREAMS):
+        relay_x.append(send(piece(p, DIAG, s, 0), rrel.at[0, s], xn))
+        relay_y.append(send(piece(p, DIAG, s, 1), rrel.at[1, s], yn))
+    build_w(YN)
+    partial(YN)
+    pair_y = pair(YN)
+    add_pair(XN, pair_x)
+    plain_x, plain_y, rich_x, rich_y = {}, {}, {}, {}
+    plain_x[0] = send(piece(p, XN, 0, 0), rx.at[0, pl.ds(0, h)], xn)
+    build_w(OWN)
+    add_pair(YN, pair_y)
+    plain_y[0] = send(piece(p, YN, 0, 1), ry.at[0, pl.ds(h, h)], yn)
+    partial(OWN)
+    pair_o = pair(OWN)
+
+    def enrich(s):
+        relay_y[s].wait_recv()
+        at = s * rows + h
+        p[XN, at:at + h] = p[XN, at:at + h] + rrel[1, s]
+        rich_x[s] = send(piece(p, XN, s, 1), rx.at[s, pl.ds(h, h)], xn)
+        relay_x[s].wait_recv()
+        at = s * rows
+        p[YN, at:at + h] = p[YN, at:at + h] + rrel[0, s]
+        rich_y[s] = send(piece(p, YN, s, 0), ry.at[s, pl.ds(0, h)], yn)
+
+    enrich(0)
+    for s in range(1, STREAMS):
+        plain_x[s] = send(piece(p, XN, s, 0), rx.at[s, pl.ds(0, h)], xn)
+        plain_y[s] = send(piece(p, YN, s, 1), ry.at[s, pl.ds(h, h)], yn)
+        enrich(s)
+    add_pair(OWN, pair_o)
+
+    padded = jnp.concatenate([ids_ref[...], jnp.zeros((k - grids, k), jnp.int32)], axis=0)
+    idst[...] = padded.T
+    build_oh(OWN)
+    build_oh(XN)
+    build_oh(YN)
+    build_oh(DIAG)
+
+    def mine(q, s, half):
+        return cc.at[q, 0, pl.ds(s * rows + half * h, h)]
+
+    got = {}
+    to_partner = {q: [] for q in range(4)}
+
+    def forward(q, s, half):
+        span = pl.ds(s * rows + half * h, h)
+        to_partner[q].append(send(cc.at[q, 0, span], cc.at[q, 1, span], partner))
+
+    for s in range(STREAMS):
+        for copy in (plain_x[s], plain_y[s], rich_x[s], rich_y[s]):
+            copy.wait_recv()
+        at = s * rows
+        cc[OWN, 0, at:at + rows] = p[OWN, at:at + rows] + rx[s] + ry[s]
+        for half in (0, 1):
+            got[XN, s, half] = send(mine(OWN, s, half), mine(XN, s, half), xn)
+            got[YN, s, 1 - half] = send(mine(OWN, s, 1 - half), mine(YN, s, 1 - half), yn)
+        span = pl.ds(at, rows)
+        to_partner[OWN].append(send(cc.at[OWN, 0, span], cc.at[OWN, 1, span], partner))
+
+    def gather(q, first):
+        for copy in to_partner[q]:
+            copy.wait_recv()
+        for other in (0, 1):
+            value = cc[q, other]
+            high = value.astype(BF16)
+            chi[other * part:(other + 1) * part] = high
+            clo[other * part:(other + 1) * part] = (value - high.astype(F32)).astype(BF16)
+        found = jnp.dot(oh[q], chi[...], preferred_element_type=F32) + jnp.dot(
+            oh[q], clo[...], preferred_element_type=F32)
+        found = found.reshape(grids, k, blk)
+        out_ref[...] = found if first else out_ref[...] + found
+
+    gather(OWN, True)
+    for s in range(STREAMS):
+        got[XN, s, 0].wait_recv()
+        got[DIAG, s, 0] = send(mine(XN, s, 0), mine(DIAG, s, 0), yn)
+        got[YN, s, 1].wait_recv()
+        got[DIAG, s, 1] = send(mine(YN, s, 1), mine(DIAG, s, 1), xn)
+        forward(XN, s, 0)
+        forward(YN, s, 1)
+        got[XN, s, 1].wait_recv()
+        forward(XN, s, 1)
+        got[YN, s, 0].wait_recv()
+        forward(YN, s, 0)
+    gather(XN, False)
+    gather(YN, False)
+    for s in range(STREAMS):
+        for half in (0, 1):
+            got[DIAG, s, half].wait_recv()
+            forward(DIAG, s, half)
+    gather(DIAG, False)
+    for copy in started:
+        copy.wait_send()
+
+
+def square(surplus, block_ids, coef):
+    grids, k, blk = surplus.shape
+    part = NBD // (SIDE * SIDE * CORES)
+    rows = part // STREAMS
+    h = rows // 2
+    slots = grids * k
+    copies = 4 + 6 * STREAMS + 4 * STREAMS + STREAMS + 2 * STREAMS + 6 * STREAMS
+    vmem = pl.BlockSpec(memory_space=pltpu.VMEM)
+    return pl.pallas_call(
+        kernel,
+        out_shape=jax.ShapeDtypeStruct(surplus.shape, F32),
+        in_specs=[vmem, pl.BlockSpec(memory_space=pltpu.SMEM), pl.BlockSpec(memory_space=pl.ANY)],
+        out_specs=vmem,
+        scratch_shapes=[
+            pltpu.VMEM((grids, k, blk), F32),
+            pltpu.VMEM((slots, blk), BF16),
+            pltpu.VMEM((slots, blk), BF16),
+            pltpu.VMEM((CORES * part, slots), BF16),
+            pltpu.VMEM((4, slots, CORES * part), BF16),
+            pltpu.VMEM((4, CORES * part, blk), F32),
+            pltpu.VMEM((4, part, blk), F32),
+            pltpu.VMEM((2, STREAMS, h, blk), F32),
+            pltpu.VMEM((STREAMS, rows, blk), F32),
+            pltpu.VMEM((STREAMS, rows, blk), F32),
+            pltpu.VMEM((4, CORES, part, blk), F32),
+            pltpu.VMEM((CORES * part, blk), BF16),
+            pltpu.VMEM((CORES * part, blk), BF16),
+            pltpu.VMEM((k, k), jnp.int32),
+            pltpu.SemaphoreType.DMA((LOADS,)),
+            pltpu.SemaphoreType.DMA((copies,)),
+            pltpu.SemaphoreType.DMA((copies,)),
+        ],
+        compiler_params=pltpu.CompilerParams(
+            collective_id=0, has_side_effects=True, vmem_limit_bytes=56 * 2**20),
+    )(block_ids, coef, surplus)
 
 
 def local(surplus, block_ids, coef):
@@ -18,8 +262,9 @@
 
 
 def solution(mesh):
+    body = square if mesh.shape["grp"] == SIDE * SIDE * CORES else local
     return jax.shard_map(
-        local,
+        body,
         mesh=mesh,
         in_specs=(P("grp", "dom", None), P("grp", "dom"), P("grp")),
         out_specs=P("grp", "dom", None),

time: 107 us -> 37.9 us (0.35)
  waiting for transfers between devices: 64.7 us -> 0 us
  Pallas kernels: 0 us -> 32.9 us
  matrix products: 27.2 us -> 0 us
  between operations: 13.4 us -> 0.01 us
  local copies, waits for them, and re-layouts: 0 us -> 4.81 us
  other arithmetic: 1.36 us -> 0 us
    psum x1 -> x0, waiting for transfers between devices: 64.6 us -> none  [local(): combined = lax.psum(partial_sum, 'grp')]
    pallas_call x0 -> x1, Pallas kernels: none -> 32.9 us  [square(): pl.pallas_call(kernel, out_shape=jax.ShapeDtypeStruct(surplus.shape, F32)...]
    dot_general x2 -> x0, matrix products: 27.2 us -> none  [the longest x1 16.8 us: local(): jnp.einsum('gkn,gkb->nb', onehot, scaled, precision=lax.Precision.HIGHEST)]
    unnamed x0 -> x1, local copies, waits for them, and re-layouts: none -> 4.81 us
  transfers between devices with their start and end apart: 1 -> 0, of which waited for: 1 -> 0; matrix products, arithmetic and copies ran while one was open for 0% -> 0% of each run, Pallas kernels for 0% -> 0%
where the time goes in v1:
time: 37.9 us; the launch traced here: 37.7 us
  Pallas kernels  32.9 us (87%)
  local copies, waits for them, and re-layouts  4.81 us (13%)
    pallas_call x1, Pallas kernels, square(): pl.pallas_call(kernel, out_shape=jax.ShapeDtypeStruct(surplus.shape, F32)...  32.9 us
    unnamed x1, local copies, waits for them, and re-layouts  4.81 us

profile of v1, /device:TPU:0, one launch (start us, length us, event | category | flops | bytes accessed | tf_op | source)
XLA Modules:
  0.0 37.7 jit_solution(6059075456517499683)
XLA Ops:
  0.0 32.9 %shard_map.37 = f32[16,128,512]{2,1,0:T(8,128)} custom-call(s32[16,128]{1,0:T(8,128)} %ids_ref.1, s32[16]{0:T(128)} %coef_ref.1, f32[16,128,512]{2,1,0:T(8,128)} %x_ref.1), custom_call_target="tpu_custom_call" | custom-call | tf_op jit(solution)/shard_map/pallas_call | solution.py:224
  32.9 4.8 %copy.5 = f32[16,128,512]{2,1,0:T(8,128)} copy(f32[16,128,512]{2,1,0:T(8,128)} %shard_map.37) | data formatting | bytes 8388608

commit v2 on v1

--- a/solution.py
+++ b/solution.py
@@ -18,7 +18,7 @@
 
 
 def kernel(ids_ref, coef_ref, x_ref, out_ref, xf, xhi, xlo, w, oh, p, rd, rrel,
-           rx, ry, cc, chi, clo, idst, load_sem, ss, rs):
+           rx, ry, cc, chl, idst, load_sem, ss, rs):
     grids, k, blk = x_ref.shape
     part = rd.shape[1]
     rows = part // STREAMS
@@ -55,7 +55,7 @@
         pl.semaphore_signal(barrier, inc=1, device_id={"grp": device}, device_id_type=MESH)
 
     row = lax.broadcasted_iota(jnp.int32, (part, k), 0)
-    lane = lax.broadcasted_iota(jnp.int32, (k, part), 1)
+    lane = lax.broadcasted_iota(jnp.int32, (k, 2 * rows), 1)
 
     def build_w(q):
         for other in (0, 1):
@@ -66,15 +66,18 @@
                 w[other * part:(other + 1) * part, g * k:(g + 1) * k] = jnp.where(hit, value, 0.0).astype(BF16)
 
     def build_oh(q):
-        for other in (0, 1):
-            shifted = lane + base(q, other)
+        for s in range(STREAMS):
+            start = jnp.where(lane < rows, base(q, 0), base(q, 1) - rows) + s * rows
+            shifted = lane + start
             for g in range(grids):
-                hit = idst[:, g:g + 1] == shifted
-                oh[q, g * k:(g + 1) * k, other * part:(other + 1) * part] = jnp.where(hit, 1.0, 0.0).astype(BF16)
-
-    def partial(q):
-        p[q] = jnp.dot(w[...], xhi[...], preferred_element_type=F32) + jnp.dot(
-            w[...], xlo[...], preferred_element_type=F32)
+                hit = jnp.where(idst[:, g:g + 1] == shifted, 1.0, 0.0).astype(BF16)
+                oh[q, s, g * k:(g + 1) * k, 0:2 * rows] = hit
+                oh[q, s, g * k:(g + 1) * k, 2 * rows:4 * rows] = hit
+
+    def half_of(q, other):
+        at = other * part
+        p[q, at:at + part] = jnp.dot(w[at:at + part], xhi[...], preferred_element_type=F32) + jnp.dot(
+            w[at:at + part], xlo[...], preferred_element_type=F32)
 
     started = []
     counter = [0]
@@ -97,8 +100,19 @@
             high = value.astype(BF16)
             xhi[g * k:(g + 1) * k, :] = high
             xlo[g * k:(g + 1) * k, :] = (value - high.astype(F32)).astype(BF16)
+        lo, hi = n * per * k, (n + 1) * per * k
+        if n < LOADS - 1:
+            term = jnp.dot(w[:, lo:hi], xhi[lo:hi], preferred_element_type=F32) + jnp.dot(
+                w[:, lo:hi], xlo[lo:hi], preferred_element_type=F32)
+            p[DIAG] = term if n == 0 else p[DIAG] + term
 
     pl.semaphore_wait(barrier, 3)
+
+    def last_term(other):
+        at, lo = other * part, (LOADS - 1) * per * k
+        p[DIAG, at:at + part] = p[DIAG, at:at + part] + (
+            jnp.dot(w[at:at + part, lo:], xhi[lo:], preferred_element_type=F32) + jnp.dot(
+                w[at:at + part, lo:], xlo[lo:], preferred_element_type=F32))
 
     def pair(q):
         return send(p.at[q, pl.ds(part, part)], rd.at[q], partner)
@@ -109,28 +123,6 @@
 
     def piece(ref, q, s, half):
         return ref.at[q, pl.ds(s * rows + half * h, h)]
-
-    partial(DIAG)
-    pair_d = pair(DIAG)
-    build_w(XN)
-    partial(XN)
-    pair_x = pair(XN)
-    add_pair(DIAG, pair_d)
-    relay_x, relay_y = [], []
-    for s in range(STREAMS):
-        relay_x.append(send(piece(p, DIAG, s, 0), rrel.at[0, s], xn))
-        relay_y.append(send(piece(p, DIAG, s, 1), rrel.at[1, s], yn))
-    build_w(YN)
-    partial(YN)
-    pair_y = pair(YN)
-    add_pair(XN, pair_x)
-    plain_x, plain_y, rich_x, rich_y = {}, {}, {}, {}
-    plain_x[0] = send(piece(p, XN, 0, 0), rx.at[0, pl.ds(0, h)], xn)
-    build_w(OWN)
-    add_pair(YN, pair_y)
-    plain_y[0] = send(piece(p, YN, 0, 1), ry.at[0, pl.ds(h, h)], yn)
-    partial(OWN)
-    pair_o = pair(OWN)
 
     def enrich(s):
         relay_y[s].wait_recv()
@@ -142,10 +134,40 @@
         p[YN, at:at + h] = p[YN, at:at + h] + rrel[0, s]
         rich_y[s] = send(piece(p, YN, s, 0), ry.at[s, pl.ds(0, h)], yn)
 
+    last_term(1)
+    pair_d = [send(p.at[DIAG, pl.ds(part + s * rows, rows)], rd.at[DIAG, pl.ds(s * rows, rows)], partner)
+              for s in range(STREAMS)]
+    last_term(0)
+    build_w(XN)
+    half_of(XN, 1)
+    pair_x = pair(XN)
+    relay_x, relay_y = [], []
+    for s in range(STREAMS):
+        pair_d[s].wait_recv()
+        at = s * rows
+        p[DIAG, at:at + rows] = p[DIAG, at:at + rows] + rd[DIAG, at:at + rows]
+        relay_x.append(send(piece(p, DIAG, s, 0), rrel.at[0, s], xn))
+        relay_y.append(send(piece(p, DIAG, s, 1), rrel.at[1, s], yn))
+    plain_x, plain_y, rich_x, rich_y = {}, {}, {}, {}
+    half_of(XN, 0)
+    add_pair(XN, pair_x)
+    plain_x[0] = send(piece(p, XN, 0, 0), rx.at[0, pl.ds(0, h)], xn)
+    build_w(YN)
+    half_of(YN, 1)
+    pair_y = pair(YN)
+    half_of(YN, 0)
+    add_pair(YN, pair_y)
+    plain_y[0] = send(piece(p, YN, 0, 1), ry.at[0, pl.ds(h, h)], yn)
+    build_w(OWN)
     enrich(0)
+    pair_o = None
     for s in range(1, STREAMS):
         plain_x[s] = send(piece(p, XN, s, 0), rx.at[s, pl.ds(0, h)], xn)
         plain_y[s] = send(piece(p, YN, s, 1), ry.at[s, pl.ds(h, h)], yn)
+        if s == 1:
+            half_of(OWN, 1)
+            pair_o = pair(OWN)
+            half_of(OWN, 0)
         enrich(s)
     add_pair(OWN, pair_o)
 
@@ -154,17 +176,16 @@
     build_oh(OWN)
     build_oh(XN)
     build_oh(YN)
-    build_oh(DIAG)
 
     def mine(q, s, half):
         return cc.at[q, 0, pl.ds(s * rows + half * h, h)]
 
     got = {}
-    to_partner = {q: [] for q in range(4)}
+    to_partner = {(q, s): [] for q in range(4) for s in range(STREAMS)}
 
     def forward(q, s, half):
         span = pl.ds(s * rows + half * h, h)
-        to_partner[q].append(send(cc.at[q, 0, span], cc.at[q, 1, span], partner))
+        to_partner[q, s].append(send(cc.at[q, 0, span], cc.at[q, 1, span], partner))
 
     for s in range(STREAMS):
         for copy in (plain_x[s], plain_y[s], rich_x[s], rich_y[s]):
@@ -175,22 +196,24 @@
             got[XN, s, half] = send(mine(OWN, s, half), mine(XN, s, half), xn)
             got[YN, s, 1 - half] = send(mine(OWN, s, 1 - half), mine(YN, s, 1 - half), yn)
         span = pl.ds(at, rows)
-        to_partner[OWN].append(send(cc.at[OWN, 0, span], cc.at[OWN, 1, span], partner))
-
-    def gather(q, first):
-        for copy in to_partner[q]:
+        to_partner[OWN, s].append(send(cc.at[OWN, 0, span], cc.at[OWN, 1, span], partner))
+
+    build_oh(DIAG)
+
+    def gather(q, s, first=False):
+        for copy in to_partner[q, s]:
             copy.wait_recv()
         for other in (0, 1):
-            value = cc[q, other]
+            value = cc[q, other, s * rows:(s + 1) * rows]
             high = value.astype(BF16)
-            chi[other * part:(other + 1) * part] = high
-            clo[other * part:(other + 1) * part] = (value - high.astype(F32)).astype(BF16)
-        found = jnp.dot(oh[q], chi[...], preferred_element_type=F32) + jnp.dot(
-            oh[q], clo[...], preferred_element_type=F32)
-        found = found.reshape(grids, k, blk)
+            at = other * rows
+            chl[at:at + rows] = high
+            chl[2 * rows + at:3 * rows + at] = (value - high.astype(F32)).astype(BF16)
+        found = jnp.dot(oh[q, s], chl[...], preferred_element_type=F32).reshape(grids, k, blk)
         out_ref[...] = found if first else out_ref[...] + found
 
-    gather(OWN, True)
+    for s in range(STREAMS):
+        gather(OWN, s, s == 0)
     for s in range(STREAMS):
         got[XN, s, 0].wait_recv()
         got[DIAG, s, 0] = send(mine(XN, s, 0), mine(DIAG, s, 0), yn)
@@ -202,13 +225,17 @@
         forward(XN, s, 1)
         got[YN, s, 0].wait_recv()
         forward(YN, s, 0)
-    gather(XN, False)
-    gather(YN, False)
+        if s < STREAMS - 1:
+            gather(XN, s)
+            gather(YN, s)
+    gather(XN, STREAMS - 1)
     for s in range(STREAMS):
         for half in (0, 1):
             got[DIAG, s, half].wait_recv()
             forward(DIAG, s, half)
-    gather(DIAG, False)
+        if s == 0:
+            gather(YN, STREAMS - 1)
+        gather(DIAG, s)
     for copy in started:
         copy.wait_send()
 
@@ -219,11 +246,11 @@
     rows = part // STREAMS
     h = rows // 2
     slots = grids * k
-    copies = 4 + 6 * STREAMS + 4 * STREAMS + STREAMS + 2 * STREAMS + 6 * STREAMS
+    copies = 3 + STREAMS + 6 * STREAMS + 4 * STREAMS + STREAMS + 2 * STREAMS + 6 * STREAMS
     vmem = pl.BlockSpec(memory_space=pltpu.VMEM)
     return pl.pallas_call(
         kernel,
-        out_shape=jax.ShapeDtypeStruct(surplus.shape, F32),
+        out_shape=pltpu.VMEM(surplus.shape, F32),
         in_specs=[vmem, pl.BlockSpec(memory_space=pltpu.SMEM), pl.BlockSpec(memory_space=pl.ANY)],
         out_specs=vmem,
         scratch_shapes=[
@@ -231,15 +258,14 @@
             pltpu.VMEM((slots, blk), BF16),
             pltpu.VMEM((slots, blk), BF16),
             pltpu.VMEM((CORES * part, slots), BF16),
-            pltpu.VMEM((4, slots, CORES * part), BF16),
+            pltpu.VMEM((4, STREAMS, slots, 4 * rows), BF16),
             pltpu.VMEM((4, CORES * part, blk), F32),
             pltpu.VMEM((4, part, blk), F32),
             pltpu.VMEM((2, STREAMS, h, blk), F32),
             pltpu.VMEM((STREAMS, rows, blk), F32),
             pltpu.VMEM((STREAMS, rows, blk), F32),
             pltpu.VMEM((4, CORES, part, blk), F32),
-            pltpu.VMEM((CORES * part, blk), BF16),
-            pltpu.VMEM((CORES * part, blk), BF16),
+            pltpu.VMEM((4 * rows, blk), BF16),
             pltpu.VMEM((k, k), jnp.int32),
             pltpu.SemaphoreType.DMA((LOADS,)),
             pltpu.SemaphoreType.DMA((copies,)),

time: 37.9 us -> 32 us (0.84)
  Pallas kernels: 32.9 us -> 29.8 us
  local copies, waits for them, and re-layouts: 4.81 us -> 2.02 us
    pallas_call x1, Pallas kernels: 32.9 us -> 29.8 us  [square(): pl.pallas_call(kernel, out_shape=pltpu.VMEM(surplus.shape, F32), in_specs...]
    unnamed x1, local copies, waits for them, and re-layouts: 4.81 us -> 2.02 us
where the time goes in v2:
time: 32 us; the launch traced here: 31.8 us
  Pallas kernels  29.8 us (93%)
  local copies, waits for them, and re-layouts  2.02 us (6%)
    pallas_call x1, Pallas kernels, square(): pl.pallas_call(kernel, out_shape=pltpu.VMEM(surplus.shape, F32), in_specs...  29.8 us
    unnamed x1, local copies, waits for them, and re-layouts  2.02 us

profile of v2, /device:TPU:0, one launch (start us, length us, event | category | flops | bytes accessed | tf_op | source)
XLA Modules:
  0.0 31.8 jit_solution(15658707667027829186)
XLA Ops:
  0.0 29.8 %shard_map.37 = f32[16,128,512]{2,1,0:T(8,128)S(1)} custom-call(s32[16,128]{1,0:T(8,128)} %ids_ref.1, s32[16]{0:T(128)} %coef_ref.1, f32[16,128,512]{2,1,0:T(8,128)} %x_ref.1), custom_call_target="tpu_custom_call" | custom-call | tf_op jit(solution)/shard_map/pallas_call | solution.py:251
  29.8 2.0 %copy.5 = f32[16,128,512]{2,1,0:T(8,128)} copy(f32[16,128,512]{2,1,0:T(8,128)S(1)} %shard_map.37) | data formatting | bytes 8388608
